TPU v7x, 32 devices: a whole 2x2x4 slice. The times are simulated.
32 devices in a mesh: dp: 4 (over x, core), head: 8 (over z, y).
Axes of the slice: x: 2, y: 2, z: 4, core: 2. Of those that a mesh axis runs over, the one named last changes fastest.
Arguments:
- tokens: bfloat16 [24576, 1152], P(('dp', 'head')), may hold values from -6 to 6
- segment_ids: int32 [24576], P('dp'), may hold values from 0 to 95, as said below
- cond: float32 [96, 1152], P('dp'), may hold values from -6 to 6
- w_ada: bfloat16 [1152, 6912], P(None, 'head'), may hold values from -0.1875 to 0.1875
- b_ada: bfloat16 [6912], P('head'), may hold values from -4 to 4
- w_qkv: bfloat16 [1152, 3, 1152], P(None, None, 'head'), may hold values from -0.1875 to 0.1875
- bias_qv: bfloat16 [2, 1152], P(None, 'head'), may hold values from -4 to 4
- w_proj: bfloat16 [1152, 1152], P('head'), may hold values from -0.75 to 0.75
- b_proj: bfloat16 [1152], replicated, may hold values from -4 to 4
- w_fc1: bfloat16 [1152, 4608], P(None, 'head'), may hold values from -0.1875 to 0.1875
- b_fc1: bfloat16 [4608], P('head'), may hold values from -4 to 4
- w_fc2: bfloat16 [4608, 1152], P('head'), may hold values from -0.09375 to 0.09375
- b_fc2: bfloat16 [1152], replicated, may hold values from -4 to 4
- cotangent: bfloat16 [24576, 1152], P(('dp', 'head')), may hold values from -6 to 6
Outputs:
- out: bfloat16 [24576, 1152], P(('dp', 'head'))
- grad_tokens: bfloat16 [24576, 1152], P(('dp', 'head'))
- grad_cond: float32 [96, 1152], P('dp')
- grad_w_ada: float32 [1152, 6912], P(None, 'head')
- grad_b_ada: float32 [6912], P('head')
- grad_w_qkv: float32 [1152, 3, 1152], P(None, None, 'head')
- grad_bias_qv: float32 [2, 1152], P(None, 'head')
- grad_w_proj: float32 [1152, 1152], P('head')
- grad_b_proj: float32 [1152], replicated
- grad_w_fc1: float32 [1152, 4608], P(None, 'head')
- grad_b_fc1: float32 [4608], P('head')
- grad_w_fc2: float32 [4608, 1152], P('head')
- grad_b_fc2: float32 [1152], replicated
Inputs may be any that keep to these rules, and one draw needn't show every extreme that they name: `segment_ids`: each packed row of 2048 consecutive tokens is two halves of 1024 tokens, each either one segment or segments of 256 tokens. The ids of the tokens of index g of dp lie in g * 24 onward; a segment's id is that base plus (its first position within those tokens) // 256, so ids never fall and some slots name no token. In the last packed row of every index of dp the first half is one segment and the second half is split.
All inputs are finite; a program needn't handle non-finite values.
Results may differ from a plain program's by a relative error of at most 0.019.
The roundings to bfloat16 on the way count: a program that leaves them out, or rounds other values in their place, can miss the bound.
Values may be sent and summed in bfloat16 or wider, within the bound.
A program may use at most 320 MiB of HBM per device.

v0:
```python
import math
import jax
import jax.numpy as jnp
from jax import lax
from jax.sharding import PartitionSpec as P

HEAD_DIM = 72
PACK = 2048
norm_eps = 1e-06
top_precision = lax.Precision.HIGHEST


def layer_norm(values):
    centered = values - jnp.mean(values, axis=-1, keepdims=True)
    inverse = lax.rsqrt(jnp.mean(centered * centered, axis=-1, keepdims=True) + norm_eps)
    return (centered * inverse, inverse)


def norm_back(grad_normed, normed, inverse):
    mean_grad = jnp.mean(grad_normed, axis=-1, keepdims=True)
    mean_cross = jnp.mean(grad_normed * normed, axis=-1, keepdims=True)
    return inverse * (grad_normed - mean_grad - normed * mean_cross)


def gelu_tanh(values):
    return jax.nn.gelu(values, approximate=True)


def block_setup(query_row, key_row, value_row, head_width):
    length, columns = query_row.shape
    heads_here = columns // head_width
    block_rows = min(512, length)
    blocks = length // block_rows
    keys_split = key_row.reshape(length, heads_here, head_width)
    values_split = value_row.reshape(length, heads_here, head_width)
    queries_split = query_row.reshape(blocks, block_rows, heads_here, head_width)
    return (block_rows, blocks, keys_split, values_split, queries_split)


def row_forward(query_row, key_row, value_row, ident_row, head_width):
    block_rows, blocks, keys_split, values_split, queries_split = block_setup(
        query_row, key_row, value_row, head_width
    )
    scale = 1.0 / math.sqrt(head_width)
    ident_blocks = ident_row.reshape(blocks, block_rows)

    def one_block(inputs):
        query_block, ident_block = inputs
        scores = (
            jnp.einsum("qhd,khd->hqk", query_block, keys_split, preferred_element_type=jnp.float32)
            * scale
        )
        allowed = (ident_block[:, None] == ident_row[None, :])[None]
        scores = jnp.where(allowed, scores, -1e30)
        highest = jnp.max(scores, axis=-1, keepdims=True)
        weights = jnp.exp(scores - highest)
        totals = jnp.sum(weights, axis=-1, keepdims=True)
        probs = (weights / totals).astype(jnp.bfloat16)
        mixed = jnp.einsum("hqk,khd->qhd", probs, values_split, preferred_element_type=jnp.float32)
        return (
            mixed.reshape(block_rows, -1).astype(jnp.bfloat16),
            (highest + jnp.log(totals))[..., 0],
        )

    mixed, log_totals = lax.map(one_block, (queries_split, ident_blocks))
    return (mixed.reshape(query_row.shape), log_totals)


def row_backward(query_row, key_row, value_row, ident_row, log_row, grad_row, head_width):
    block_rows, blocks, keys_split, values_split, queries_split = block_setup(
        query_row, key_row, value_row, head_width
    )
    heads_here = keys_split.shape[1]
    scale = 1.0 / math.sqrt(head_width)
    grads_split = grad_row.reshape(blocks, block_rows, heads_here, head_width)
    ident_blocks = ident_row.reshape(blocks, block_rows)

    def one_block(carry, inputs):
        key_total, value_total = carry
        query_block, grad_block, ident_block, log_block = inputs
        scores = (
            jnp.einsum("qhd,khd->hqk", query_block, keys_split, preferred_element_type=jnp.float32)
            * scale
        )
        allowed = (ident_block[:, None] == ident_row[None, :])[None]
        probs = jnp.where(allowed, jnp.exp(scores - log_block[:, :, None]), 0.0)
        grad_probs = jnp.einsum(
            "qhd,khd->hqk", grad_block, values_split, preferred_element_type=jnp.float32
        )
        inner = jnp.sum(probs * grad_probs, axis=-1, keepdims=True)
        grad_scores = (probs * (grad_probs - inner)).astype(jnp.bfloat16)
        grad_query = (
            jnp.einsum("hqk,khd->qhd", grad_scores, keys_split, preferred_element_type=jnp.float32)
            * scale
        )
        key_total = (
            key_total
            + jnp.einsum(
                "hqk,qhd->khd", grad_scores, query_block, preferred_element_type=jnp.float32
            )
            * scale
        )
        value_total = value_total + jnp.einsum(
            "hqk,qhd->khd",
            probs.astype(jnp.bfloat16),
            grad_block,
            preferred_element_type=jnp.float32,
        )
        return ((key_total, value_total), grad_query.reshape(block_rows, -1).astype(jnp.bfloat16))

    zero_total = jnp.zeros(keys_split.shape, jnp.float32)
    (key_total, value_total), grad_query = lax.scan(
        one_block, (zero_total, zero_total), (queries_split, grads_split, ident_blocks, log_row)
    )
    length = ident_row.shape[0]
    return (
        grad_query.reshape(length, -1),
        key_total.reshape(length, -1).astype(jnp.bfloat16),
        value_total.reshape(length, -1).astype(jnp.bfloat16),
    )


def attend(query, keys, values, idents):
    packed = idents.shape[0] // PACK

    def one_row(inputs):
        return row_forward(inputs[0], inputs[1], inputs[2], inputs[3], HEAD_DIM)

    mixed, log_totals = lax.map(
        one_row,
        (
            query.reshape(packed, PACK, -1),
            keys.reshape(packed, PACK, -1),
            values.reshape(packed, PACK, -1),
            idents.reshape(packed, PACK),
        ),
    )
    return (mixed.reshape(query.shape), log_totals)


def attend_back(query, keys, values, idents, log_totals, grad_mix):
    packed = idents.shape[0] // PACK

    def one_row(inputs):
        return row_backward(
            inputs[0], inputs[1], inputs[2], inputs[3], inputs[4], inputs[5], HEAD_DIM
        )

    grad_query, grad_key, grad_value = lax.map(
        one_row,
        (
            query.reshape(packed, PACK, -1),
            keys.reshape(packed, PACK, -1),
            values.reshape(packed, PACK, -1),
            idents.reshape(packed, PACK),
            log_totals,
            grad_mix.reshape(packed, PACK, -1),
        ),
    )
    return (
        grad_query.reshape(query.shape),
        grad_key.reshape(query.shape),
        grad_value.reshape(query.shape),
    )


def local(
    tokens,
    segment_ids,
    cond,
    w_ada,
    b_ada,
    w_qkv,
    bias_qv,
    w_proj,
    b_proj,
    w_fc1,
    b_fc1,
    w_fc2,
    b_fc2,
    cotangent,
):
    rows_here, width = tokens.shape
    slots = cond.shape[0]
    columns = w_qkv.shape[2]
    row_start = lax.axis_index("head") * rows_here
    own_ids = (
        lax.dynamic_slice_in_dim(segment_ids, row_start, rows_here) - lax.axis_index("dp") * slots
    )
    pick = (own_ids[:, None] == jnp.arange(slots, dtype=jnp.int32)[None, :]).astype(jnp.float32)
    cond_act, silu_back = jax.vjp(jax.nn.silu, cond)
    cond_low = cond_act.astype(jnp.bfloat16)
    mod_part = jnp.dot(cond_low, w_ada, preferred_element_type=jnp.float32) + b_ada.astype(
        jnp.float32
    )
    modulation = lax.all_gather(mod_part, "head", axis=1, tiled=True)
    per_token = jnp.dot(pick, modulation, precision=top_precision)
    shift_a, scale_a, gate_a, shift_m, scale_m, gate_m = jnp.split(per_token, 6, axis=1)
    resid = tokens.astype(jnp.float32)
    normed_a, inverse_a = layer_norm(resid)
    attn_in = (normed_a * (1.0 + scale_a) + shift_a).astype(jnp.bfloat16)
    gathered_a = lax.all_gather(attn_in, "head", axis=0, tiled=True)
    qkv_weight = w_qkv.reshape(width, 3 * columns)
    qkv_bias = jnp.concatenate(
        [bias_qv[0], jnp.zeros((columns,), bias_qv.dtype), bias_qv[1]]
    ).astype(jnp.float32)
    qkv = (jnp.dot(gathered_a, qkv_weight, preferred_element_type=jnp.float32) + qkv_bias).astype(
        jnp.bfloat16
    )
    query = qkv[:, :columns]
    keys = qkv[:, columns : 2 * columns]
    values = qkv[:, 2 * columns :]
    attn_mix, log_totals = attend(query, keys, values, segment_ids)
    branch_a = lax.psum_scatter(
        jnp.dot(attn_mix, w_proj, preferred_element_type=jnp.float32),
        "head",
        scatter_dimension=0,
        tiled=True,
    ) + b_proj.astype(jnp.float32)
    mid = resid + gate_a * branch_a
    normed_m, inverse_m = layer_norm(mid)
    mlp_in = (normed_m * (1.0 + scale_m) + shift_m).astype(jnp.bfloat16)
    cotan = cotangent.astype(jnp.float32)
    grad_branch_m = (gate_m * cotan).astype(jnp.bfloat16)
    gathered_m = lax.all_gather(mlp_in, "head", axis=0, tiled=True)
    pre = jnp.dot(gathered_m, w_fc1, preferred_element_type=jnp.float32) + b_fc1.astype(jnp.float32)
    hidden, gelu_back = jax.vjp(gelu_tanh, pre)
    hidden_low = hidden.astype(jnp.bfloat16)
    branch_m = lax.psum_scatter(
        jnp.dot(hidden_low, w_fc2, preferred_element_type=jnp.float32).astype(jnp.bfloat16),
        "head",
        scatter_dimension=0,
        tiled=True,
    ).astype(jnp.float32) + b_fc2.astype(jnp.float32)
    grad_rows_m = lax.all_gather(grad_branch_m, "head", axis=0, tiled=True)
    grad_hidden = jnp.einsum("td,fd->tf", grad_rows_m, w_fc2, preferred_element_type=jnp.float32)
    grad_pre = gelu_back(grad_hidden)[0].astype(jnp.bfloat16)
    grad_fc1 = jnp.einsum("td,tf->df", gathered_m, grad_pre, preferred_element_type=jnp.float32)
    grad_fc2 = jnp.einsum("tf,td->fd", hidden_low, grad_rows_m, preferred_element_type=jnp.float32)
    grad_b1 = jnp.sum(grad_pre.astype(jnp.float32), axis=0)
    grad_mlp_in = lax.psum_scatter(
        jnp.einsum("tf,df->td", grad_pre, w_fc1, preferred_element_type=jnp.float32),
        "head",
        scatter_dimension=0,
        tiled=True,
    )
    output = (mid + gate_m * branch_m).astype(jnp.bfloat16)
    grad_mid = cotan + norm_back(grad_mlp_in * (1.0 + scale_m), normed_m, inverse_m)
    grad_branch_a = (gate_a * grad_mid).astype(jnp.bfloat16)
    grad_rows_a = lax.all_gather(grad_branch_a, "head", axis=0, tiled=True)
    grad_proj = jnp.einsum("tc,td->cd", attn_mix, grad_rows_a, preferred_element_type=jnp.float32)
    grad_mix = jnp.einsum(
        "td,cd->tc", grad_rows_a, w_proj, preferred_element_type=jnp.float32
    ).astype(jnp.bfloat16)
    grad_query, grad_key, grad_value = attend_back(
        query, keys, values, segment_ids, log_totals, grad_mix
    )
    grad_qkv = jnp.concatenate([grad_query, grad_key, grad_value], axis=1)
    grad_w_qkv = jnp.einsum(
        "td,tc->dc", gathered_a, grad_qkv, preferred_element_type=jnp.float32
    ).reshape(width, 3, columns)
    grad_bias_qv = jnp.stack(
        [
            jnp.sum(grad_query.astype(jnp.float32), axis=0),
            jnp.sum(grad_value.astype(jnp.float32), axis=0),
        ]
    )
    grad_attn_in = lax.psum_scatter(
        jnp.einsum("tc,dc->td", grad_qkv, qkv_weight, preferred_element_type=jnp.float32).astype(
            jnp.bfloat16
        ),
        "head",
        scatter_dimension=0,
        tiled=True,
    ).astype(jnp.float32)
    grad_tokens = (
        grad_mid + norm_back(grad_attn_in * (1.0 + scale_a), normed_a, inverse_a)
    ).astype(jnp.bfloat16)
    per_token_grad = jnp.concatenate(
        [
            grad_attn_in,
            grad_attn_in * normed_a,
            grad_mid * branch_a,
            grad_mlp_in,
            grad_mlp_in * normed_m,
            cotan * branch_m,
        ],
        axis=1,
    )
    grad_mod_part = jnp.einsum("ts,tm->sm", pick, per_token_grad, precision=top_precision)
    grad_mod = lax.psum_scatter(
        grad_mod_part.astype(jnp.bfloat16), "head", scatter_dimension=1, tiled=True
    ).astype(jnp.float32)
    grad_w_ada = jnp.einsum(
        "sd,sm->dm", cond_low.astype(jnp.float32), grad_mod, precision=top_precision
    )
    grad_b_ada = jnp.sum(grad_mod, axis=0)
    grad_cond_part = jnp.einsum(
        "sm,dm->sd", grad_mod, w_ada.astype(jnp.float32), precision=top_precision
    )
    proj_bias_part = jnp.sum(grad_branch_a.astype(jnp.float32), axis=0)
    mlp_bias_part = jnp.sum(grad_branch_m.astype(jnp.float32), axis=0)
    grad_cond_act, grad_b_proj, grad_b2 = (
        lax.psum(grad_cond_part.astype(jnp.bfloat16), "head").astype(jnp.float32),
        lax.psum(proj_bias_part.astype(jnp.bfloat16), "head").astype(jnp.float32),
        lax.psum(mlp_bias_part.astype(jnp.bfloat16), "head").astype(jnp.float32),
    )
    grad_cond = silu_back(grad_cond_act)[0]
    summed = (
        lax.psum(grad_w_ada.astype(jnp.bfloat16), "dp").astype(jnp.float32),
        lax.psum(grad_b_ada.astype(jnp.bfloat16), "dp").astype(jnp.float32),
        lax.psum(grad_w_qkv.astype(jnp.bfloat16), "dp").astype(jnp.float32),
        lax.psum(grad_bias_qv.astype(jnp.bfloat16), "dp").astype(jnp.float32),
        lax.psum(grad_proj.astype(jnp.bfloat16), "dp").astype(jnp.float32),
        lax.psum(grad_b_proj.astype(jnp.bfloat16), "dp").astype(jnp.float32),
        lax.psum(grad_fc1.astype(jnp.bfloat16), "dp").astype(jnp.float32),
        lax.psum(grad_b1.astype(jnp.bfloat16), "dp").astype(jnp.float32),
        lax.psum(grad_fc2.astype(jnp.bfloat16), "dp").astype(jnp.float32),
        lax.psum(grad_b2.astype(jnp.bfloat16), "dp").astype(jnp.float32),
    )
    return (output, grad_tokens, grad_cond) + tuple(summed)


def solution(mesh):
    placed = (
        P(("dp", "head"), None),
        P("dp"),
        P("dp", None),
        P(None, "head"),
        P("head"),
        P(None, None, "head"),
        P(None, "head"),
        P("head", None),
        P(),
        P(None, "head"),
        P("head"),
        P("head", None),
        P(),
        P(("dp", "head"), None),
    )
    return jax.shard_map(
        local,
        mesh=mesh,
        in_specs=placed,
        out_specs=(
            P(("dp", "head"), None),
            P(("dp", "head"), None),
            P("dp", None),
            P(None, "head"),
            P("head"),
            P(None, None, "head"),
            P(None, "head"),
            P("head", None),
            P(),
            P(None, "head"),
            P("head"),
            P("head", None),
            P(),
        ),
        check_vma=False,
    )
```

profile of v0, /device:TPU:0, one launch (start us, length us, event | category | flops | bytes accessed | tf_op | source)
XLA Modules:
  0.0 2927.3 jit_solution(12163566460413241053)
XLA Ops:
  12.7 33.5 %all-gather = f32[8,864,24]{1,2,0:T(8,128)S(1)} all-gather(f32[1,864,24]{1,2,0:T(8,128)S(1)} %fusion.64), channel_id=1, replica_groups=mesh['dp'=4,'head'=8] {'head'}, dimensions={0}, use_global_device_ids=true | all-gather | bytes 746496 | tf_op jit(solution)/shard_map/all_gather | solution.py:196
  64.5 11.4 reduce-scatter.8.cloned.1.call-start
  76.1 184.8 %all-gather.6.cloned.1.call-done = bf16[6144,1152]{1,0:T(8,128)(2,1)} async-done(((bf16[768,1152]{1,0:T(8,128)(2,1)}), bf16[6144,1152]{1,0:T(8,128)(2,1)}) %all-gather.6.cloned.1.call-update) | async-done | bytes 14155792 | tf_op jit(solution)/shard_map/all_gather | solution.py:202
  260.9 10.3 add_convert_fusion
  277.1 140.8 %while.54 = (s32[]{:T(128)}, bf16[3,2048,144]{2,1,0:T(8,128)(2,1)}, f32[3,4,2,512]{3,2,1,0:T(2,128)}, bf16[3,2048,144]{1,2,0:T(8,128)(2,1)}, s32[3,2048]{1,0:T(4...) while((s32[]{:T(128)}, bf16[3,2048,144]{2,1,0:T(8,128)(2,1)}, ...), condition=%wide.region_7.8_spmd, body=%wide.region_2.7_spmd.sunk | while | flops 630266880 | bytes 39967056 | solution.py:129
  282.1 38.9 %while.57 = (s32[]{:T(128)}, bf16[4,512,144]{1,2,0:T(8,128)(2,1)}, f32[4,2,512]{2,1,0:T(2,128)S(1)}, s32[4,512]{1,0:T(4,128)S(1)}, s32[2048]{0:T(1024)S(1)}, /*i...) while((s32[]{:T(128)}, bf16[4,512,144]{1,2,0:T(8,128)(2,1)}, ...), condition=%wide.region_6.6_spmd, body=%wide.region_3.5_spmd.sunk | while | flops 630266880 | bytes 31176820 | solution.py:65
  329.0 38.9 %while.57 = (s32[]{:T(128)}, bf16[4,512,144]{1,2,0:T(8,128)(2,1)}, f32[4,2,512]{2,1,0:T(2,128)S(1)}, s32[4,512]{1,0:T(4,128)S(1)}, s32[2048]{0:T(1024)S(1)}, /*i...) while((s32[]{:T(128)}, bf16[4,512,144]{1,2,0:T(8,128)(2,1)}, ...), condition=%wide.region_6.6_spmd, body=%wide.region_3.5_spmd.sunk | while | flops 630266880 | bytes 31176820 | solution.py:65
  375.9 38.9 %while.57 = (s32[]{:T(128)}, bf16[4,512,144]{1,2,0:T(8,128)(2,1)}, f32[4,2,512]{2,1,0:T(2,128)S(1)}, s32[4,512]{1,0:T(4,128)S(1)}, s32[2048]{0:T(1024)S(1)}, /*i...) while((s32[]{:T(128)}, bf16[4,512,144]{1,2,0:T(8,128)(2,1)}, ...), condition=%wide.region_6.6_spmd, body=%wide.region_3.5_spmd.sunk | while | flops 630266880 | bytes 31176820 | solution.py:65
  417.8 15.5 fusion.85
  434.0 445.9 %reduce-scatter.8.cloned.1.call-done = f32[768,1152]{1,0:T(8,128)} async-done(((f32[6144,1152]{1,0:T(8,128)}), f32[768,1152]{1,0:T(8,128)}) %reduce-scatter.8.cloned.1.call-update) | async-done | bytes 3538960 | tf_op jit(solution)/shard_map/reduce_scatter | solution.py:214
  896.0 189.6 %all-gather.8.cloned.1.call-done = bf16[6144,1152]{1,0:T(8,128)(2,1)} async-done(((bf16[768,1152]{1,0:T(8,128)(2,1)}), bf16[6144,1152]{1,0:T(8,128)(2,1)}) %all-gather.8.cloned.1.call-update) | async-done | bytes 14155792 | tf_op jit(solution)/shard_map/all_gather | solution.py:225
  1085.7 16.1 fusion.86
  1101.8 20.9 convolution_convert_fusion.1
  1122.8 159.0 %all-gather.10.cloned.1.call-done = bf16[6144,1152]{1,0:T(8,128)(2,1)} async-done(((bf16[768,1152]{1,0:T(8,128)(2,1)}), bf16[6144,1152]{1,0:T(8,128)(2,1)}) %all-gather.10.cloned.1.call-update) | async-done | bytes 14155792 | tf_op jit(solution)/shard_map/all_gather | solution.py:235
  1281.8 24.4 fusion.78
  1306.2 20.0 fusion.87
  1326.9 186.0 %reduce-scatter.10.cloned.1.call-done = bf16[768,1152]{1,0:T(8,128)(2,1)} async-done(((bf16[6144,1152]{1,0:T(8,128)(2,1)}), bf16[768,1152]{1,0:T(8,128)(2,1)}) %reduce-scatter.10.cloned.1.call-update) | async-done | bytes 1769488 | tf_op jit(solution)/shard_map/reduce_scatter | solution.py:229
  1512.9 451.3 %reduce-scatter.12.cloned.1.call-done = f32[768,1152]{1,0:T(8,128)} async-done(((f32[6144,1152]{1,0:T(8,128)}), f32[768,1152]{1,0:T(8,128)}) %reduce-scatter.12.cloned.1.call-update) | async-done | bytes 3538960 | tf_op jit(solution)/shard_map/reduce_scatter | solution.py:241
  1979.2 194.5 %all-gather.12.cloned.1.call-done = bf16[6144,1152]{1,0:T(8,128)(2,1)} async-done(((bf16[768,1152]{1,0:T(8,128)(2,1)}), bf16[6144,1152]{1,0:T(8,128)(2,1)}) %all-gather.12.cloned.1.call-update) | async-done | bytes 14155792 | tf_op jit(solution)/shard_map/all_gather | solution.py:250
  2186.5 265.0 %while.56 = (s32[]{:T(128)}, bf16[3,2048,144]{2,1,0:T(8,128)(2,1)}, bf16[3,2048,144]{1,2,0:T(8,128)(2,1)}, bf16[3,2048,144]{1,2,0:T(8,128)(2,1)}, bf16[3,2048,14...) while((s32[]{:T(128)}, bf16[3,2048,144]{2,1,0:T(8,128)(2,1)}, ...), condition=%wide.region_19.20_spmd, body=%wide.region_15.19_spmd.sunk | while | flops 1544666112 | bytes 114133608 | solution.py:149
  2205.0 63.7 %while.58 = (s32[]{:T(128)}, f32[2048,2,72]{0,2,1:T(8,128)}, f32[2048,2,72]{0,2,1:T(8,128)}, bf16[4,512,144]{1,2,0:T(8,128)(2,1)}, bf16[4,512,2,72]{1,3,2,0:T(8,...) while((s32[]{:T(128)}, f32[2048,2,72]{0,2,1:T(8,128)}, ...), condition=%wide.region_18.18_spmd.clone, body=%wide.region_16.17_spmd.clone.sunk | while | flops 1544076288 | bytes 95906112 | solution.py:112
  2293.2 63.8 %while.58 = (s32[]{:T(128)}, f32[2048,2,72]{0,2,1:T(8,128)}, f32[2048,2,72]{0,2,1:T(8,128)}, bf16[4,512,144]{1,2,0:T(8,128)(2,1)}, bf16[4,512,2,72]{1,3,2,0:T(8,...) while((s32[]{:T(128)}, f32[2048,2,72]{0,2,1:T(8,128)}, ...), condition=%wide.region_18.18_spmd.clone, body=%wide.region_16.17_spmd.clone.sunk | while | flops 1544076288 | bytes 95906112 | solution.py:112
  2381.4 63.8 %while.58 = (s32[]{:T(128)}, f32[2048,2,72]{0,2,1:T(8,128)}, f32[2048,2,72]{0,2,1:T(8,128)}, bf16[4,512,144]{1,2,0:T(8,128)(2,1)}, bf16[4,512,2,72]{1,3,2,0:T(8,...) while((s32[]{:T(128)}, f32[2048,2,72]{0,2,1:T(8,128)}, ...), condition=%wide.region_18.18_spmd.clone, body=%wide.region_16.17_spmd.clone.sunk | while | flops 1544076288 | bytes 95906112 | solution.py:112
  2461.8 11.1 convolution_convert_fusion
  2473.0 14.7 convolution_convert_fusion.5
  2487.8 20.8 convolution_convert_fusion.6
  2508.6 10.8 convolution_convert_fusion.7
  2519.4 181.3 %reduce-scatter.14.cloned.1.call-done = bf16[768,1152]{1,0:T(8,128)(2,1)} async-done(((bf16[6144,1152]{1,0:T(8,128)(2,1)}), bf16[768,1152]{1,0:T(8,128)(2,1)}) %reduce-scatter.14.cloned.1.call-update) | async-done | bytes 1769488 | tf_op jit(solution)/shard_map/reduce_scatter | solution.py:268
  2735.3 56.6 %reduce-scatter.16.cloned.1.call-done = bf16[864,24]{1,0:T(8,128)(2,1)} async-done(((bf16[6912,24]{1,0:T(8,128)(2,1)}), bf16[864,24]{1,0:T(8,128)(2,1)}) %reduce-scatter.16.cloned.1.call-update) | async-done | bytes 41488
  2800.0 35.5 %all-reduce = (bf16[24,1152]{1,0:T(8,128)(2,1)S(1)}, bf16[1152]{0:T(1024)(128)(2,1)S(1)}, bf16[1152]{0:T(1024)(128)(2,1)S(1)}) all-reduce(bf16[24,1152]{1,0:T(8,128)(2,1)S(1)} %convolution_convert_fusion.9, bf16[1152]{0:T(1024)(128)(2,1)S(1)} %copy-done.49, bf16[1152]{0:T(1024)(128)(2,1)S(1)} %copy-done.48), channel_id=1, replica_groups=mesh['dp'=4,'head'=8] {'head'}, use_global_device_ids=true, to_apply=%region_24.25 | all-reduce | flops 29952 | bytes 119808 | tf_op jit(solution)/shard_map/psum | solution.py:304
  2835.6 11.8 all-reduce.1
  2851.1 58.4 %all-reduce.5.cloned.1.call-done = (bf16[1152,864]{0,1:T(8,128)(2,1)}, bf16[1152,3,144]{0,2,1:T(8,128)(2,1)}, bf16[144,1152]{1,0:T(8,128)(2,1)}, bf16[1152,576]{0,1:T(8,128)(2,1)}, bf16[576,1152]{1,0:T(8,128)(2,1)}) async-done(((bf16[1152,864]{0,1:T(8,128)(2,1)}, bf16[1152,3,144]{0,2,1:T(8,128)(2,1)}, bf16[144,1152]{1,0:T(8,128)(2,1)}, bf16[1152,576]{0,1:T(8,128)(2,1)}, bf16[576,1152]{1,0:T(8,128)(2,1)}), ...) | async-done | bytes 5971984 | tf_op jit(solution)/shard_map/psum | solution.py:310
  (620 shorter events, 545.5 us)
Async XLA Ops:
  7.2 253.7 %all-gather.6.cloned.1.call-start = ((), (), s32[]{:S(2)}) async-start(), calls=%async_computation.5 | async-start | bytes 15925248 | tf_op jit(solution)/shard_map/all_gather | solution.py:202
  9.9 45.5 %copy-start.37 = (f32[768]{0:T(1024)}, f32[768]{0:T(1024)S(1)}, u32[]{:S(2)}) copy-start(f32[768]{0:T(1024)S(1)} %broadcast_multiply_fusion.5) | copy-start | bytes 9220
  9.9 36.8 %copy-start.47 = (s32[6144]{0:T(1024)S(1)}, s32[6144]{0:T(1024)}, u32[]{:S(2)}) copy-start(s32[6144]{0:T(1024)} %param.23) | copy-start | bytes 73732
  12.0 43.4 %copy-start.45 = (f32[768]{0:T(1024)}, f32[768]{0:T(1024)S(1)}, u32[]{:S(2)}) copy-start(f32[768]{0:T(1024)S(1)} %add_rsqrt_fusion.1) | copy-start | bytes 9220
  46.7 15.7 copy-start.8
  62.4 13.5 copy-start.54
  62.4 198.5 %copy-start.58 = (bf16[1152,3,144]{0,2,1:T(8,128)(2,1)S(1)}, bf16[1152,3,144]{0,2,1:T(8,128)(2,1)}, u32[]{:S(2)}) copy-start(bf16[1152,3,144]{0,2,1:T(8,128)(2,1)} %param.27) | copy-start | bytes 2985988
  64.5 815.5 %reduce-scatter.8.cloned.1.call-start = ((), (), s32[]{:S(2)}) async-start(), calls=%async_computation.6 | async-start | bytes 31850496 | tf_op jit(solution)/shard_map/reduce_scatter | solution.py:214
  417.8 15.5 copy-start.31
  433.4 652.3 %all-gather.8.cloned.1.call-start = ((), (), s32[]{:S(2)}) async-start(), calls=%async_computation.7 | async-start | bytes 15925248 | tf_op jit(solution)/shard_map/all_gather | solution.py:225
  434.0 450.2 %copy-start.41 = (f32[1152]{0:T(1024)}, f32[1152]{0:T(1024)S(1)}, u32[]{:S(2)}) copy-start(f32[1152]{0:T(1024)S(1)} %convert_element_type.224) | copy-start | bytes 13828
  884.2 1087.7 %copy-start.35 = (f32[768]{0:T(1024)}, f32[768]{0:T(1024)S(1)}, u32[]{:S(2)}) copy-start(f32[768]{0:T(1024)S(1)} %broadcast_multiply_fusion.4) | copy-start | bytes 9220
  886.0 1085.9 %copy-start.39 = (f32[768]{0:T(1024)}, f32[768]{0:T(1024)S(1)}, u32[]{:S(2)}) copy-start(f32[768]{0:T(1024)S(1)} %add_rsqrt_fusion) | copy-start | bytes 9220
  891.1 390.6 %all-gather.10.cloned.1.call-start = ((), (), s32[]{:S(2)}) async-start(), calls=%async_computation.9 | async-start | bytes 15925248 | tf_op jit(solution)/shard_map/all_gather | solution.py:235
  896.0 616.9 %reduce-scatter.10.cloned.1.call-start = ((), (), s32[]{:S(2)}) async-start(), calls=%async_computation.8 | async-start | bytes 15925248 | tf_op jit(solution)/shard_map/reduce_scatter | solution.py:229
  896.0 385.7 %copy-start.52 = (f32[576]{0:T(1024)}, f32[576]{0:T(1024)S(1)}, u32[]{:S(2)}) copy-start(f32[576]{0:T(1024)S(1)} %convert_element_type.226) | copy-start | bytes 6916
  1085.7 16.1 copy-start.57
  1122.7 841.4 %reduce-scatter.12.cloned.1.call-start = ((), (), s32[]{:S(2)}) async-start(), calls=%async_computation.10 | async-start | bytes 31850496 | tf_op jit(solution)/shard_map/reduce_scatter | solution.py:241
  1326.2 847.4 %all-gather.12.cloned.1.call-start = ((), (), s32[]{:S(2)}) async-start(), calls=%async_computation.11 | async-start | bytes 15925248 | tf_op jit(solution)/shard_map/all_gather | solution.py:250
  1326.9 645.0 %copy-start.43 = (f32[1152]{0:T(1024)}, f32[1152]{0:T(1024)S(1)}, u32[]{:S(2)}) copy-start(f32[1152]{0:T(1024)S(1)} %convert_element_type.230) | copy-start | bytes 13828
  1973.0 200.7 %copy-start.32 = (bf16[144,1152]{1,0:T(8,128)(2,1)S(1)}, bf16[144,1152]{1,0:T(8,128)(2,1)}, u32[]{:S(2)}) copy-start(bf16[144,1152]{1,0:T(8,128)(2,1)} %param.29) | copy-start | bytes 995332
  1979.1 721.6 %reduce-scatter.14.cloned.1.call-start = ((), (), s32[]{:S(2)}) async-start(), calls=%async_computation.12 | async-start | bytes 15925248 | tf_op jit(solution)/shard_map/reduce_scatter | solution.py:268
  2472.9 14.8 copy-start.53
  2473.0 319.0 %reduce-scatter.16.cloned.1.call-start = ((), (), s32[]{:S(2)}) async-start(), calls=%async_computation.13 | async-start | bytes 1990656
  2487.8 20.8 copy-start.21
  2487.8 20.8 copy-start.23
  2487.8 20.8 copy-start.25
  2519.4 183.2 %copy-start.38 = (f32[768]{0:T(1024)S(1)}, f32[768]{0:T(1024)}, u32[]{:S(2)}) copy-start(f32[768]{0:T(1024)} %copy-done.37) | copy-start | bytes 9220
  2519.4 183.2 %copy-start.46 = (f32[768]{0:T(1024)S(1)}, f32[768]{0:T(1024)}, u32[]{:S(2)}) copy-start(f32[768]{0:T(1024)} %copy-done.45) | copy-start | bytes 9220
  2726.0 65.9 %copy-start.30 = (f32[24,1152]{1,0:T(8,128)S(1)}, f32[24,1152]{1,0:T(8,128)}, u32[]{:S(2)}) copy-start(f32[24,1152]{1,0:T(8,128)} %param.24) | copy-start | bytes 331780
  2726.0 183.5 %all-reduce.5.cloned.1.call-start = ((), (), s32[]{:S(2)}) async-start(), calls=%async_computation.14 | async-start | bytes 11943936 | tf_op jit(solution)/shard_map/psum | solution.py:310
  2794.9 40.8 %copy-start.56 = (bf16[576]{0:T(1024)(128)(2,1)S(1)}, bf16[576]{0:T(1024)(128)(2,1)}, u32[]{:S(2)}) copy-start(bf16[576]{0:T(1024)(128)(2,1)} %get-tuple-element.468) | copy-start | bytes 3460
  (93 other events, 257.9 us)
Sparse Core Ops, SparseCore 0:
  64.6 196.2 all-gather.5
  433.5 446.4 reduce-scatter.7
  891.2 194.3 all-gather.7
  1088.3 193.4 all-gather.9
  1285.3 227.5 reduce-scatter.9
  1516.6 447.4 reduce-scatter.11
  1979.2 194.3 all-gather.11
  2473.1 227.5 reduce-scatter.13
  2726.1 65.7 reduce-scatter.15
  2795.6 113.8 all-reduce.4
where the time goes:
time: 2940 us; the launch traced here: 2930 us
  waiting for transfers between devices  2110 us (72%)
  matrix products  411 us (14%)
  other arithmetic  152 us (5%)
  local copies, waits for them, and re-layouts  147 us (5%)
  blocking collectives  80.8 us (3%)
    reduce_scatter x1, waiting for transfers between devices, local(): lax.psum_scatter(jnp.einsum('tf,df->td', grad_pre, w_fc1, preferred_eleme...  451 us
    reduce_scatter x1, waiting for transfers between devices, local(): lax.psum_scatter(jnp.dot(attn_mix, w_proj, preferred_element_type=jnp.flo...  446 us
    all_gather x1, waiting for transfers between devices, local(): grad_rows_a = lax.all_gather(grad_branch_a, 'head', axis=0, tiled=True)  194 us
    all_gather x1, waiting for transfers between devices, local(): gathered_m = lax.all_gather(mlp_in, 'head', axis=0, tiled=True)  190 us
    reduce_scatter x1, waiting for transfers between devices, local(): lax.psum_scatter(jnp.dot(hidden_low, w_fc2, preferred_element_type=jnp.fl...  186 us
    all_gather x1, waiting for transfers between devices, local(): gathered_a = lax.all_gather(attn_in, 'head', axis=0, tiled=True)  185 us
    reduce_scatter x1, waiting for transfers between devices, local(): lax.psum_scatter(jnp.einsum('tc,dc->td', grad_qkv, qkv_weight, preferred_...  181 us
    all_gather x1, waiting for transfers between devices, local(): grad_rows_m = lax.all_gather(grad_branch_m, 'head', axis=0, tiled=True)  159 us
  transfers between devices with their start and end apart: 10, of which 10 were waited for; matrix products, arithmetic and copies ran while one was open for 5% of the time, Pallas kernels for 0%

commit v1 on v0

--- a/solution.py
+++ b/solution.py
@@ -1,3 +1,4 @@
+import functools
 import math
 import jax
 import jax.numpy as jnp
@@ -8,6 +9,29 @@
 PACK = 2048
 norm_eps = 1e-06
 top_precision = lax.Precision.HIGHEST
+
+
+def store_the_indices(raw, net_axis):
+    vals = []
+    cores_n = jax.lax.axis_size(net_axis)
+    for tick in range(cores_n):
+        vals.append((tick, (tick + 1) % cores_n))
+    grid = []
+    for tick in range(cores_n):
+        grid.append((tick, (tick - 1) % cores_n))
+    lower, w1 = ([raw], [raw])
+    for _ in range(cores_n // 2):
+        odd = jax.lax.ppermute(lower[-1], net_axis, vals)
+        lower.append(odd)
+    for _ in range((cores_n - 1) // 2):
+        z_new = jax.lax.ppermute(w1[-1], net_axis, grid)
+        w1.append(z_new)
+    part_now = jnp.concatenate([*lower[::-1], *w1[1:]], 0)
+    t1 = jax.lax.axis_index(net_axis)
+    return jnp.roll(part_now, (t1 - cores_n // 2) * raw.shape[0], 0)
+
+
+_lift_state = functools.partial(store_the_indices, net_axis="head")
 
 
 def layer_norm(values):
@@ -247,7 +271,7 @@
     output = (mid + gate_m * branch_m).astype(jnp.bfloat16)
     grad_mid = cotan + norm_back(grad_mlp_in * (1.0 + scale_m), normed_m, inverse_m)
     grad_branch_a = (gate_a * grad_mid).astype(jnp.bfloat16)
-    grad_rows_a = lax.all_gather(grad_branch_a, "head", axis=0, tiled=True)
+    grad_rows_a = _lift_state(grad_branch_a)
     grad_proj = jnp.einsum("tc,td->cd", attn_mix, grad_rows_a, preferred_element_type=jnp.float32)
     grad_mix = jnp.einsum(
         "td,cd->tc", grad_rows_a, w_proj, preferred_element_type=jnp.float32

time: 2940 us -> 3050 us (1.037)
  starting transfers between devices: 11.8 us -> 99.4 us
  local copies, waits for them, and re-layouts: 147 us -> 181 us
    all_gather x1 -> x0, waiting for transfers between devices: 194 us -> none  [local(): grad_rows_a = lax.all_gather(grad_branch_a, 'head', axis=0, tiled=True)]
    ppermute x0 -> x7, waiting for transfers between devices: none -> 186 us  [the longest x4 186 us: store_the_indices(): odd = jax.lax.ppermute(lower[-1], net_axis, vals)]
    ppermute x0 -> x7, starting transfers between devices: none -> 87.7 us  [the longest x3 81.1 us: store_the_indices(): z_new = jax.lax.ppermute(w1[-1], net_axis, grid)]
    unnamed x113 -> x138, local copies, waits for them, and re-layouts: 18.1 us -> 50.6 us
  transfers between devices with their start and end apart: 10 -> 16, of which waited for: 10 -> 14; matrix products, arithmetic and copies ran while one was open for 5% -> 6% of each run, Pallas kernels for 0% -> 0%
where the time goes in v1:
time: 3050 us; the launch traced here: 3040 us
  waiting for transfers between devices  2100 us (69%)
  matrix products  414 us (14%)
  local copies, waits for them, and re-layouts  181 us (6%)
  other arithmetic  152 us (5%)
  starting transfers between devices  99.4 us (3%)
  blocking collectives  80.5 us (3%)
    reduce_scatter x1, waiting for transfers between devices, local(): lax.psum_scatter(jnp.einsum('tf,df->td', grad_pre, w_fc1, preferred_eleme...  451 us
    reduce_scatter x1, waiting for transfers between devices, local(): lax.psum_scatter(jnp.dot(attn_mix, w_proj, preferred_element_type=jnp.flo...  446 us
    reduce_scatter x1, waiting for transfers between devices, local(): lax.psum_scatter(jnp.einsum('tc,dc->td', grad_qkv, qkv_weight, preferred_...  193 us
    all_gather x1, waiting for transfers between devices, local(): gathered_m = lax.all_gather(mlp_in, 'head', axis=0, tiled=True)  190 us
    reduce_scatter x1, waiting for transfers between devices, local(): lax.psum_scatter(jnp.dot(hidden_low, w_fc2, preferred_element_type=jnp.fl...  188 us
    ppermute x4, waiting for transfers between devices, store_the_indices(): odd = jax.lax.ppermute(lower[-1], net_axis, vals)  186 us
    all_gather x1, waiting for transfers between devices, local(): gathered_a = lax.all_gather(attn_in, 'head', axis=0, tiled=True)  185 us
    all_gather x1, waiting for transfers between devices, local(): grad_rows_m = lax.all_gather(grad_branch_m, 'head', axis=0, tiled=True)  159 us
  transfers between devices with their start and end apart: 16, of which 14 were waited for; matrix products, arithmetic and copies ran while one was open for 6% of the time, Pallas kernels for 0%

profile of v1, /device:TPU:0, one launch (start us, length us, event | category | flops | bytes accessed | tf_op | source)
XLA Modules:
  0.0 3040.8 jit_solution(17746104285116108183)
XLA Ops:
  12.7 33.5 %all-gather = f32[8,864,24]{1,2,0:T(8,128)S(1)} all-gather(f32[1,864,24]{1,2,0:T(8,128)S(1)} %fusion.74), channel_id=1, replica_groups=mesh['dp'=4,'head'=8] {'head'}, dimensions={0}, use_global_device_ids=true | all-gather | bytes 746496 | tf_op jit(solution)/shard_map/all_gather | solution.py:220
  76.1 184.8 %all-gather.5.cloned.1.call-done = bf16[6144,1152]{1,0:T(8,128)(2,1)} async-done(((bf16[768,1152]{1,0:T(8,128)(2,1)}), bf16[6144,1152]{1,0:T(8,128)(2,1)}) %all-gather.5.cloned.1.call-update) | async-done | bytes 14155792 | tf_op jit(solution)/shard_map/all_gather | solution.py:226
  277.1 140.9 %while.54 = (s32[]{:T(128)}, bf16[3,2048,144]{2,1,0:T(8,128)(2,1)}, f32[3,4,2,512]{3,2,1,0:T(2,128)}, bf16[3,2048,144]{1,2,0:T(8,128)(2,1)}, s32[3,2048]{1,0:T(4...) while((s32[]{:T(128)}, bf16[3,2048,144]{2,1,0:T(8,128)(2,1)}, ...), condition=%wide.region_7.8_spmd, body=%wide.region_2.7_spmd.sunk | while | flops 630266880 | bytes 39967056 | solution.py:153
  282.1 38.9 %while.57 = (s32[]{:T(128)}, bf16[4,512,144]{1,2,0:T(8,128)(2,1)}, f32[4,2,512]{2,1,0:T(2,128)S(1)}, s32[4,512]{1,0:T(4,128)S(1)}, s32[2048]{0:T(1024)S(1)}, /*i...) while((s32[]{:T(128)}, bf16[4,512,144]{1,2,0:T(8,128)(2,1)}, ...), condition=%wide.region_6.6_spmd, body=%wide.region_3.5_spmd.sunk | while | flops 630266880 | bytes 31176820 | solution.py:89
  329.1 38.9 %while.57 = (s32[]{:T(128)}, bf16[4,512,144]{1,2,0:T(8,128)(2,1)}, f32[4,2,512]{2,1,0:T(2,128)S(1)}, s32[4,512]{1,0:T(4,128)S(1)}, s32[2048]{0:T(1024)S(1)}, /*i...) while((s32[]{:T(128)}, bf16[4,512,144]{1,2,0:T(8,128)(2,1)}, ...), condition=%wide.region_6.6_spmd, body=%wide.region_3.5_spmd.sunk | while | flops 630266880 | bytes 31176820 | solution.py:89
  376.1 38.9 %while.57 = (s32[]{:T(128)}, bf16[4,512,144]{1,2,0:T(8,128)(2,1)}, f32[4,2,512]{2,1,0:T(2,128)S(1)}, s32[4,512]{1,0:T(4,128)S(1)}, s32[2048]{0:T(1024)S(1)}, /*i...) while((s32[]{:T(128)}, bf16[4,512,144]{1,2,0:T(8,128)(2,1)}, ...), condition=%wide.region_6.6_spmd, body=%wide.region_3.5_spmd.sunk | while | flops 630266880 | bytes 31176820 | solution.py:89
  418.0 15.5 fusion.97
  434.2 446.0 %reduce-scatter.8.cloned.1.call-done = f32[768,1152]{1,0:T(8,128)} async-done(((f32[6144,1152]{1,0:T(8,128)}), f32[768,1152]{1,0:T(8,128)}) %reduce-scatter.8.cloned.1.call-update) | async-done | bytes 3538960 | tf_op jit(solution)/shard_map/reduce_scatter | solution.py:238
  896.2 189.6 %all-gather.7.cloned.1.call-done = bf16[6144,1152]{1,0:T(8,128)(2,1)} async-done(((bf16[768,1152]{1,0:T(8,128)(2,1)}), bf16[6144,1152]{1,0:T(8,128)(2,1)}) %all-gather.7.cloned.1.call-update) | async-done | bytes 14155792 | tf_op jit(solution)/shard_map/all_gather | solution.py:249
  1085.8 16.2 fusion.98
  1102.0 20.9 convolution_convert_fusion.1
  1123.0 158.9 %all-gather.9.cloned.1.call-done = bf16[6144,1152]{1,0:T(8,128)(2,1)} async-done(((bf16[768,1152]{1,0:T(8,128)(2,1)}), bf16[6144,1152]{1,0:T(8,128)(2,1)}) %all-gather.9.cloned.1.call-update) | async-done | bytes 14155792 | tf_op jit(solution)/shard_map/all_gather | solution.py:259
  1281.9 24.0 fusion.90
  1306.0 18.6 fusion.99
  1325.2 187.8 %reduce-scatter.10.cloned.1.call-done = bf16[768,1152]{1,0:T(8,128)(2,1)} async-done(((bf16[6144,1152]{1,0:T(8,128)(2,1)}), bf16[768,1152]{1,0:T(8,128)(2,1)}) %reduce-scatter.10.cloned.1.call-update) | async-done | bytes 1769488 | tf_op jit(solution)/shard_map/reduce_scatter | solution.py:253
  1513.0 451.3 %reduce-scatter.12.cloned.1.call-done = f32[768,1152]{1,0:T(8,128)} async-done(((f32[6144,1152]{1,0:T(8,128)}), f32[768,1152]{1,0:T(8,128)}) %reduce-scatter.12.cloned.1.call-update) | async-done | bytes 3538960 | tf_op jit(solution)/shard_map/reduce_scatter | solution.py:265
  1980.4 41.5 %collective-permute-done = bf16[768,1152]{1,0:T(8,128)(2,1)S(1)} collective-permute-done((bf16[768,1152]{1,0:T(8,128)(2,1)S(1)}, bf16[768,1152]{1,0:T(8,128)(2,1)S(1)}, u32[]{:S(2)}, u32[]{:S(2)}) %collective-permute-start) | collective-permute-done | bytes 1769504 | tf_op jit(solution)/shard_map/ppermute | solution.py:24
  2026.8 70.2 %collective-permute-done.1 = bf16[768,1152]{1,0:T(8,128)(2,1)S(1)} collective-permute-done((bf16[768,1152]{1,0:T(8,128)(2,1)S(1)}, bf16[768,1152]{1,0:T(8,128)(2,1)S(1)}, u32[]{:S(2)}, u32[]{:S(2)}) %collective-permute-start.1) | collective-permute-done | bytes 1769504 | tf_op jit(solution)/shard_map/ppermute | solution.py:24
  2099.6 37.5 %collective-permute-start.5 = (bf16[768,1152]{1,0:T(8,128)(2,1)}, bf16[768,1152]{1,0:T(8,128)(2,1)}, u32[]{:S(2)}, u32[]{:S(2)}) collective-permute-start(bf16[768,1152]{1,0:T(8,128)(2,1)} %collective-permute-done.4), channel_id=1, source_target_pairs={{0,7},{1,0},{2,1},{3,2},{4,3},{5,4},{6,5},{7,6},{8,15},{9,8},{10,9... | collective-permute-start | bytes 5308424 | tf_op jit(solution)/shard_map/ppermute | solution.py:27
  2137.1 37.6 %collective-permute-done.2 = bf16[768,1152]{1,0:T(8,128)(2,1)} collective-permute-done((bf16[768,1152]{1,0:T(8,128)(2,1)S(1)}, bf16[768,1152]{1,0:T(8,128)(2,1)}, u32[]{:S(2)}, u32[]{:S(2)}) %collective-permute-start.2) | collective-permute-done | bytes 1769504 | tf_op jit(solution)/shard_map/ppermute | solution.py:24
  2177.3 38.7 %collective-permute-start.6 = (bf16[768,1152]{1,0:T(8,128)(2,1)}, bf16[768,1152]{1,0:T(8,128)(2,1)S(1)}, u32[]{:S(2)}, u32[]{:S(2)}) collective-permute-start(bf16[768,1152]{1,0:T(8,128)(2,1)} %collective-permute-done.5), channel_id=1, source_target_pairs={{0,7},{1,0},{2,1},{3,2},{4,3},{5,4},{6,5},{7,6},{8,15},{9,8},{10,9... | collective-permute-start | bytes 5308424 | tf_op jit(solution)/shard_map/ppermute | solution.py:27
  2216.0 36.4 %collective-permute-done.3 = bf16[768,1152]{1,0:T(8,128)(2,1)} collective-permute-done((bf16[768,1152]{1,0:T(8,128)(2,1)}, bf16[768,1152]{1,0:T(8,128)(2,1)}, u32[]{:S(2)}, u32[]{:S(2)}) %collective-permute-start.3) | collective-permute-done | bytes 1769504 | tf_op jit(solution)/shard_map/ppermute | solution.py:24
  2299.4 265.4 %while.56 = (s32[]{:T(128)}, bf16[3,2048,144]{2,1,0:T(8,128)(2,1)}, bf16[3,2048,144]{1,2,0:T(8,128)(2,1)}, bf16[3,2048,144]{1,2,0:T(8,128)(2,1)}, bf16[3,2048,14...) while((s32[]{:T(128)}, bf16[3,2048,144]{2,1,0:T(8,128)(2,1)}, ...), condition=%wide.region_19.20_spmd, body=%wide.region_15.19_spmd.sunk | while | flops 1544666112 | bytes 114133608 | solution.py:173
  2318.0 63.9 %while.58 = (s32[]{:T(128)}, f32[2048,2,72]{0,2,1:T(8,128)}, f32[2048,2,72]{0,2,1:T(8,128)}, bf16[4,512,144]{1,2,0:T(8,128)(2,1)}, bf16[4,512,2,72]{1,3,2,0:T(8,...) while((s32[]{:T(128)}, f32[2048,2,72]{0,2,1:T(8,128)}, ...), condition=%wide.region_18.18_spmd.clone, body=%wide.region_16.17_spmd.clone.sunk | while | flops 1544076288 | bytes 95906112 | solution.py:136
  2406.2 63.9 %while.58 = (s32[]{:T(128)}, f32[2048,2,72]{0,2,1:T(8,128)}, f32[2048,2,72]{0,2,1:T(8,128)}, bf16[4,512,144]{1,2,0:T(8,128)(2,1)}, bf16[4,512,2,72]{1,3,2,0:T(8,...) while((s32[]{:T(128)}, f32[2048,2,72]{0,2,1:T(8,128)}, ...), condition=%wide.region_18.18_spmd.clone, body=%wide.region_16.17_spmd.clone.sunk | while | flops 1544076288 | bytes 95906112 | solution.py:136
  2494.5 63.9 %while.58 = (s32[]{:T(128)}, f32[2048,2,72]{0,2,1:T(8,128)}, f32[2048,2,72]{0,2,1:T(8,128)}, bf16[4,512,144]{1,2,0:T(8,128)(2,1)}, bf16[4,512,2,72]{1,3,2,0:T(8,...) while((s32[]{:T(128)}, f32[2048,2,72]{0,2,1:T(8,128)}, ...), condition=%wide.region_18.18_spmd.clone, body=%wide.region_16.17_spmd.clone.sunk | while | flops 1544076288 | bytes 95906112 | solution.py:136
  2586.2 14.8 convolution_convert_fusion.4
  2601.0 20.6 convolution_convert_fusion.5
  2621.6 193.3 %reduce-scatter.14.cloned.1.call-done = bf16[768,1152]{1,0:T(8,128)(2,1)} async-done(((bf16[6144,1152]{1,0:T(8,128)(2,1)}), bf16[768,1152]{1,0:T(8,128)(2,1)}) %reduce-scatter.14.cloned.1.call-update) | async-done | bytes 1769488 | tf_op jit(solution)/shard_map/reduce_scatter | solution.py:292
  2865.4 40.8 %reduce-scatter.16.cloned.1.call-done = bf16[864,24]{1,0:T(8,128)(2,1)} async-done(((bf16[6912,24]{1,0:T(8,128)(2,1)}), bf16[864,24]{1,0:T(8,128)(2,1)}) %reduce-scatter.16.cloned.1.call-update) | async-done | bytes 41488
  2914.3 35.2 %all-reduce = (bf16[24,1152]{1,0:T(8,128)(2,1)S(1)}, bf16[1152]{0:T(1024)(128)(2,1)S(1)}, bf16[1152]{0:T(1024)(128)(2,1)S(1)}) all-reduce(bf16[24,1152]{1,0:T(8,128)(2,1)S(1)} %convolution_convert_fusion.7, bf16[1152]{0:T(1024)(128)(2,1)S(1)} %copy-done.53, bf16[1152]{0:T(1024)(128)(2,1)S(1)} %copy-done.52), channel_id=1, replica_groups=mesh['dp'=4,'head'=8] {'head'}, use_global_device_ids=true, to_apply=%region_24.25 | all-reduce | flops 29952 | bytes 119808 | tf_op jit(solution)/shard_map/psum | solution.py:328
  2965.1 58.3 %all-reduce.5.cloned.1.call-done = (bf16[1152,864]{0,1:T(8,128)(2,1)}, bf16[1152,3,144]{0,2,1:T(8,128)(2,1)}, bf16[144,1152]{1,0:T(8,128)(2,1)}, bf16[1152,576]{0,1:T(8,128)(2,1)}, bf16[576,1152]{1,0:T(8,128)(2,1)}) async-done(((bf16[1152,864]{0,1:T(8,128)(2,1)}, bf16[1152,3,144]{0,2,1:T(8,128)(2,1)}, bf16[144,1152]{1,0:T(8,128)(2,1)}, bf16[1152,576]{0,1:T(8,128)(2,1)}, bf16[576,1152]{1,0:T(8,128)(2,1)}), ...) | async-done | bytes 5971984 | tf_op jit(solution)/shard_map/psum | solution.py:334
  (657 shorter events, 651.6 us)
Async XLA Ops:
  7.2 253.7 %all-gather.5.cloned.1.call-start = ((), (), s32[]{:S(2)}) async-start(), calls=%async_computation.5 | async-start | bytes 15925248 | tf_op jit(solution)/shard_map/all_gather | solution.py:226
  9.9 45.5 %copy-start.41 = (f32[768]{0:T(1024)}, f32[768]{0:T(1024)S(1)}, u32[]{:S(2)}) copy-start(f32[768]{0:T(1024)S(1)} %broadcast_multiply_fusion.5) | copy-start | bytes 9220
  12.0 43.4 %copy-start.49 = (f32[768]{0:T(1024)}, f32[768]{0:T(1024)S(1)}, u32[]{:S(2)}) copy-start(f32[768]{0:T(1024)S(1)} %add_rsqrt_fusion.1) | copy-start | bytes 9220
  62.4 198.5 %copy-start.63 = (bf16[1152,3,144]{0,2,1:T(8,128)(2,1)S(1)}, bf16[1152,3,144]{0,2,1:T(8,128)(2,1)}, u32[]{:S(2)}) copy-start(bf16[1152,3,144]{0,2,1:T(8,128)(2,1)} %param.27) | copy-start | bytes 2985988
  64.5 815.6 %reduce-scatter.8.cloned.1.call-start = ((), (), s32[]{:S(2)}) async-start(), calls=%async_computation.6 | async-start | bytes 31850496 | tf_op jit(solution)/shard_map/reduce_scatter | solution.py:238
  433.5 652.3 %all-gather.7.cloned.1.call-start = ((), (), s32[]{:S(2)}) async-start(), calls=%async_computation.7 | async-start | bytes 15925248 | tf_op jit(solution)/shard_map/all_gather | solution.py:249
  434.2 450.2 %copy-start.45 = (f32[1152]{0:T(1024)}, f32[1152]{0:T(1024)S(1)}, u32[]{:S(2)}) copy-start(f32[1152]{0:T(1024)S(1)} %convert_element_type.224) | copy-start | bytes 13828
  884.4 1087.7 %copy-start.39 = (f32[768]{0:T(1024)}, f32[768]{0:T(1024)S(1)}, u32[]{:S(2)}) copy-start(f32[768]{0:T(1024)S(1)} %broadcast_multiply_fusion.4) | copy-start | bytes 9220
  886.2 1085.9 %copy-start.43 = (f32[768]{0:T(1024)}, f32[768]{0:T(1024)S(1)}, u32[]{:S(2)}) copy-start(f32[768]{0:T(1024)S(1)} %add_rsqrt_fusion) | copy-start | bytes 9220
  891.3 390.6 %all-gather.9.cloned.1.call-start = ((), (), s32[]{:S(2)}) async-start(), calls=%async_computation.9 | async-start | bytes 15925248 | tf_op jit(solution)/shard_map/all_gather | solution.py:259
  896.2 616.9 %reduce-scatter.10.cloned.1.call-start = ((), (), s32[]{:S(2)}) async-start(), calls=%async_computation.8 | async-start | bytes 15925248 | tf_op jit(solution)/shard_map/reduce_scatter | solution.py:253
  896.2 385.7 %copy-start.56 = (f32[576]{0:T(1024)}, f32[576]{0:T(1024)S(1)}, u32[]{:S(2)}) copy-start(f32[576]{0:T(1024)S(1)} %convert_element_type.226) | copy-start | bytes 6916
  896.2 205.8 %copy-start.61 = (bf16[576,1152]{1,0:T(8,128)(2,1)S(1)}, bf16[576,1152]{1,0:T(8,128)(2,1)}, u32[]{:S(2)}) copy-start(bf16[576,1152]{1,0:T(8,128)(2,1)} %param.33) | copy-start | bytes 3981316
  1123.0 841.3 %reduce-scatter.12.cloned.1.call-start = ((), (), s32[]{:S(2)}) async-start(), calls=%async_computation.10 | async-start | bytes 31850496 | tf_op jit(solution)/shard_map/reduce_scatter | solution.py:265
  1324.6 1490.4 %reduce-scatter.14.cloned.1.call-start = ((), (), s32[]{:S(2)}) async-start(), calls=%async_computation.11 | async-start | bytes 15925248 | tf_op jit(solution)/shard_map/reduce_scatter | solution.py:292
  1325.2 646.8 %copy-start.47 = (f32[1152]{0:T(1024)}, f32[1152]{0:T(1024)S(1)}, u32[]{:S(2)}) copy-start(f32[1152]{0:T(1024)S(1)} %convert_element_type.230) | copy-start | bytes 13828
  1978.9 43.0 %copy-start.17 = (bf16[768,1152]{1,0:T(8,128)(2,1)}, bf16[768,1152]{1,0:T(8,128)(2,1)S(1)}, u32[]{:S(2)}) copy-start(bf16[768,1152]{1,0:T(8,128)(2,1)S(1)} %get-tuple-element.473) | copy-start | bytes 5308420
  1978.9 43.0 %collective-permute-start = (bf16[768,1152]{1,0:T(8,128)(2,1)S(1)}, bf16[768,1152]{1,0:T(8,128)(2,1)S(1)}, u32[]{:S(2)}, u32[]{:S(2)}) collective-permute-start(bf16[768,1152]{1,0:T(8,128)(2,1)S(1)} %get-tuple-element.473), channel_id=1, source_target_pairs={{0,1},{1,2},{2,3},{3,4},{4,5},{5,6},{6,7},{7,0},{8,9},{9,10},{10,1... | collective-permute-start | bytes 5308424 | tf_op jit(solution)/shard_map/ppermute | solution.py:24
  2021.9 77.7 %copy-start.22 = (bf16[768,1152]{1,0:T(8,128)(2,1)}, bf16[768,1152]{1,0:T(8,128)(2,1)S(1)}, u32[]{:S(2)}) copy-start(bf16[768,1152]{1,0:T(8,128)(2,1)S(1)} %collective-permute-done) | copy-start | bytes 5308420
  2021.9 75.1 %collective-permute-start.1 = (bf16[768,1152]{1,0:T(8,128)(2,1)S(1)}, bf16[768,1152]{1,0:T(8,128)(2,1)S(1)}, u32[]{:S(2)}, u32[]{:S(2)}) collective-permute-start(bf16[768,1152]{1,0:T(8,128)(2,1)S(1)} %collective-permute-done), channel_id=1, source_target_pairs={{0,1},{1,2},{2,3},{3,4},{4,5},{5,6},{6,7},{7,0},{8,9},{9,10},{10,1... | collective-permute-start | bytes 5308424 | tf_op jit(solution)/shard_map/ppermute | solution.py:24
  2021.9 77.7 %collective-permute-start.4 = (bf16[768,1152]{1,0:T(8,128)(2,1)S(1)}, bf16[768,1152]{1,0:T(8,128)(2,1)}, u32[]{:S(2)}, u32[]{:S(2)}) collective-permute-start(bf16[768,1152]{1,0:T(8,128)(2,1)S(1)} %get-tuple-element.473), channel_id=1, source_target_pairs={{0,7},{1,0},{2,1},{3,2},{4,3},{5,4},{6,5},{7,6},{8,15},{9,8},{10,9... | collective-permute-start | bytes 5308424 | tf_op jit(solution)/shard_map/ppermute | solution.py:27
  2097.0 77.7 %collective-permute-start.2 = (bf16[768,1152]{1,0:T(8,128)(2,1)S(1)}, bf16[768,1152]{1,0:T(8,128)(2,1)}, u32[]{:S(2)}, u32[]{:S(2)}) collective-permute-start(bf16[768,1152]{1,0:T(8,128)(2,1)S(1)} %collective-permute-done.1), channel_id=1, source_target_pairs={{0,1},{1,2},{2,3},{3,4},{4,5},{5,6},{6,7},{7,0},{8,9},{9,10},{10,1... | collective-permute-start | bytes 5308424 | tf_op jit(solution)/shard_map/ppermute | solution.py:24
  2099.6 77.7 %collective-permute-start.5 = (bf16[768,1152]{1,0:T(8,128)(2,1)}, bf16[768,1152]{1,0:T(8,128)(2,1)}, u32[]{:S(2)}, u32[]{:S(2)}) collective-permute-start(bf16[768,1152]{1,0:T(8,128)(2,1)} %collective-permute-done.4), channel_id=1, source_target_pairs={{0,7},{1,0},{2,1},{3,2},{4,3},{5,4},{6,5},{7,6},{8,15},{9,8},{10,9... | collective-permute-start | bytes 5308424 | tf_op jit(solution)/shard_map/ppermute | solution.py:27
  2174.7 77.7 %collective-permute-start.3 = (bf16[768,1152]{1,0:T(8,128)(2,1)}, bf16[768,1152]{1,0:T(8,128)(2,1)}, u32[]{:S(2)}, u32[]{:S(2)}) collective-permute-start(bf16[768,1152]{1,0:T(8,128)(2,1)} %collective-permute-done.2), channel_id=1, source_target_pairs={{0,1},{1,2},{2,3},{3,4},{4,5},{5,6},{6,7},{7,0},{8,9},{9,10},{10,1... | collective-permute-start | bytes 5308424 | tf_op jit(solution)/shard_map/ppermute | solution.py:24
  2177.3 80.9 %copy-start.25 = (bf16[768,1152]{1,0:T(8,128)(2,1)S(1)}, bf16[768,1152]{1,0:T(8,128)(2,1)}, u32[]{:S(2)}) copy-start(bf16[768,1152]{1,0:T(8,128)(2,1)} %copy-done.24) | copy-start | bytes 5308420
  2177.3 90.7 %collective-permute-start.6 = (bf16[768,1152]{1,0:T(8,128)(2,1)}, bf16[768,1152]{1,0:T(8,128)(2,1)S(1)}, u32[]{:S(2)}, u32[]{:S(2)}) collective-permute-start(bf16[768,1152]{1,0:T(8,128)(2,1)} %collective-permute-done.5), channel_id=1, source_target_pairs={{0,7},{1,0},{2,1},{3,2},{4,3},{5,4},{6,5},{7,6},{8,15},{9,8},{10,9... | collective-permute-start | bytes 5308424 | tf_op jit(solution)/shard_map/ppermute | solution.py:27
  2586.2 320.0 %reduce-scatter.16.cloned.1.call-start = ((), (), s32[]{:S(2)}) async-start(), calls=%async_computation.12 | async-start | bytes 1990656
  2621.6 195.2 %copy-start.42 = (f32[768]{0:T(1024)S(1)}, f32[768]{0:T(1024)}, u32[]{:S(2)}) copy-start(f32[768]{0:T(1024)} %copy-done.41) | copy-start | bytes 9220
  2621.6 195.2 %copy-start.50 = (f32[768]{0:T(1024)S(1)}, f32[768]{0:T(1024)}, u32[]{:S(2)}) copy-start(f32[768]{0:T(1024)} %copy-done.49) | copy-start | bytes 9220
  2840.2 183.1 %all-reduce.5.cloned.1.call-start = ((), (), s32[]{:S(2)}) async-start(), calls=%async_computation.13 | async-start | bytes 11943936 | tf_op jit(solution)/shard_map/psum | solution.py:334
  2855.0 51.2 %copy-start.34 = (f32[24,1152]{1,0:T(8,128)S(1)}, f32[24,1152]{1,0:T(8,128)}, u32[]{:S(2)}) copy-start(f32[24,1152]{1,0:T(8,128)} %param.24) | copy-start | bytes 331780
  2909.2 40.5 %copy-start.60 = (bf16[576]{0:T(1024)(128)(2,1)S(1)}, bf16[576]{0:T(1024)(128)(2,1)}, u32[]{:S(2)}) copy-start(bf16[576]{0:T(1024)(128)(2,1)} %get-tuple-element.468) | copy-start | bytes 3460
  (104 other events, 444.8 us)
Sparse Core Ops, SparseCore 0:
  64.6 196.2 all-gather.4
  433.6 446.4 reduce-scatter.7
  891.4 194.3 all-gather.6
  1088.4 193.4 all-gather.8
  1285.4 227.5 reduce-scatter.9
  1516.8 447.4 reduce-scatter.11
  2586.3 228.6 reduce-scatter.13
  2840.4 65.7 reduce-scatter.15
  2909.5 113.7 all-reduce.4
